TPU v7x, 32 devices: a whole 2x2x4 slice. The times are simulated.
32 devices in a mesh: seq: 8 (over z, y), ch: 4 (over x, core).
Axes of the slice: x: 2, y: 2, z: 4, core: 2. Of those that a mesh axis runs over, the one named last changes fastest.
Arguments:
- query_proj: float32 [64, 8192], P('ch', 'seq'), may hold values from -6 to 6
- key_proj: float32 [64, 8192], P('ch', 'seq'), may hold values from -6 to 6
- value_proj: float32 [64, 8192], P('ch', 'seq'), may hold values from -6 to 6
- filter_taps: float32 [64, 8192], P('ch', 'seq'), may hold values from -6 to 6
- out_cotangent: float32 [64, 8192], P('ch', 'seq'), may hold values from -6 to 6
Outputs:
- hyena_out: float32 [64, 8192], P('ch', 'seq')
- query_grad: float32 [64, 8192], P('ch', 'seq')
- key_grad: float32 [64, 8192], P('ch', 'seq')
- value_grad: float32 [64, 8192], P('ch', 'seq')
- filter_grad: float32 [64, 8192], P('ch', 'seq')
All inputs are finite; a program needn't handle non-finite values.
Results may differ from a plain program's by a relative error of at most 0.000098.
Values sent between devices are 32-bit elements; how exact they have to be, the bound alone decides.
No kernel may reach another device: no remote copies, remote signals or barrier semaphores. Data moves between devices by JAX's collectives and lax.ppermute only.
A program may use at most 64 MiB of HBM per device.

v0:
```python
import math

import jax
import jax.numpy as jnp
import numpy as np
from jax import lax
from jax.experimental import pallas as pl
from jax.experimental.pallas import tpu as pltpu
from jax.sharding import PartitionSpec as P

FAC = 512
LANES = 128
SUBLANES = 8


exact_mode = lax.Precision.HIGHEST


def angle_grid(row_ids, col_ids, period):
    angles = (row_ids * col_ids % period).astype(jnp.float32) * (2.0 * math.pi / period)
    return (jnp.cos(angles), jnp.sin(angles))


def index_grid(row_count, col_count):
    return (
        lax.broadcasted_iota(jnp.int32, (row_count, col_count), 0),
        lax.broadcasted_iota(jnp.int32, (row_count, col_count), 1),
    )


def grad_items(first_grad, second_grad):
    return ([first_grad, second_grad], False)


def bins_over_devices(query_proj, key_proj, value_proj, filter_taps, out_cotangent):
    devices = lax.axis_size("seq")
    position = lax.axis_index("seq")
    channels = filter_taps.shape[0]
    tokens = filter_taps.shape[1]
    run_count = tokens // FAC
    half_first = run_count * devices
    first_len = 2 * half_first
    col_group = FAC // devices
    full_len = first_len * FAC
    width_cg = channels * col_group
    out_scale = 1.0 / (full_len * math.sqrt(tokens * devices))
    slot_count = first_len // devices
    time_ids, bin_ids = index_grid(half_first, first_len)
    cos_first, sin_first = angle_grid(time_ids, bin_ids, first_len)
    fwd_imag = -sin_first
    inv_imag = -sin_first
    bin_rows, lane_ids = index_grid(first_len, width_cg)
    cos_turn, sin_turn = angle_grid(bin_rows, position * col_group + lane_ids % col_group, full_len)
    square_rows, square_cols = index_grid(FAC, FAC)
    cos_second, sin_second = angle_grid(square_rows, square_cols, FAC)
    cos_grid = cos_second.reshape(devices, col_group, FAC)
    sin_grid = sin_second.reshape(devices, col_group, FAC)
    cos_back = cos_second.reshape(FAC, devices, col_group)
    sin_back = sin_second.reshape(FAC, devices, col_group)

    def product(left, right, conjugate):
        left_real, left_imag = (left[0], left[1])
        if conjugate:
            left_imag = -left_imag
        real_part = left_real * right[0] - left_imag * right[1]
        imag_part = left_real * right[1] + left_imag * right[0]
        return jnp.stack([real_part, imag_part])

    gated = key_proj * value_proj
    weighted = out_cotangent * query_proj
    slabs = jnp.stack([gated, filter_taps, weighted])
    item_count = slabs.shape[0]
    blocks = slabs.reshape(item_count, channels, run_count, devices, col_group).transpose(
        0, 3, 2, 1, 4
    )
    blocks = blocks.reshape(item_count, devices, run_count, width_cg)
    received = lax.all_to_all(blocks, "seq", split_axis=1, concat_axis=1, tiled=True)
    item_count = received.shape[0]
    flattened = received.reshape(item_count, half_first, width_cg)
    real_sum = jnp.einsum("stm,tk->skm", flattened, cos_first, precision=exact_mode)
    imag_sum = jnp.einsum("stm,tk->skm", flattened, fwd_imag, precision=exact_mode)
    turned_real = real_sum * cos_turn + imag_sum * sin_turn
    turned_imag = imag_sum * cos_turn - real_sum * sin_turn
    stacked = jnp.stack([turned_real, turned_imag], axis=1)
    turned = stacked.reshape(item_count, 2, devices, slot_count, width_cg)
    received = lax.all_to_all(turned, "seq", split_axis=2, concat_axis=2, tiled=True)
    item_count = received.shape[0]
    slots_here = received.shape[3]
    pieces = received.reshape(item_count, 2, devices, slots_here, channels, col_group)

    def contract(values, matrix):
        return jnp.einsum("snkcg,ngq->skcq", values, matrix, precision=exact_mode)

    real_out = contract(pieces[:, 0], cos_grid) + contract(pieces[:, 1], sin_grid)
    imag_out = contract(pieces[:, 1], cos_grid) - contract(pieces[:, 0], sin_grid)
    spectra = jnp.stack([real_out, imag_out], axis=1)
    gated_spec, filter_spec, weighted_spec = (spectra[0], spectra[1], spectra[2])
    forward_prod = product(filter_spec, gated_spec, False)
    grad_list, paired = grad_items(
        product(filter_spec, weighted_spec, True), product(gated_spec, weighted_spec, True)
    )
    spectra = jnp.stack([forward_prod] + grad_list, axis=0)
    item_count = spectra.shape[0]

    def contract(values, matrix):
        return jnp.einsum("skcq,qng->skncg", values, matrix, precision=exact_mode)

    real_out = contract(spectra[:, 0], cos_back) - contract(spectra[:, 1], sin_back)
    imag_out = contract(spectra[:, 0], sin_back) + contract(spectra[:, 1], cos_back)
    columns = jnp.stack([real_out, imag_out], axis=1).reshape(
        item_count, 2, slot_count, devices, width_cg
    )
    received = lax.all_to_all(columns, "seq", split_axis=3, concat_axis=2, tiled=True)
    item_count = received.shape[0]
    flattened = received.reshape(item_count, 2, first_len, width_cg)
    rows_real = flattened[:, 0]
    rows_imag = flattened[:, 1]
    turned_real = rows_real * cos_turn - rows_imag * sin_turn
    turned_imag = rows_imag * cos_turn + rows_real * sin_turn

    def contract(values, matrix):
        return jnp.einsum("skm,tk->stm", values, matrix, precision=exact_mode)

    real_out = contract(turned_real, cos_first) + contract(turned_imag, inv_imag)
    turned = real_out
    item_count = turned.shape[0]
    sending = turned.reshape(item_count, devices, run_count, width_cg)
    returned = lax.all_to_all(sending, "seq", split_axis=1, concat_axis=1, tiled=True)
    returned = returned.reshape(item_count, devices, run_count, channels, col_group).transpose(
        0, 3, 2, 1, 4
    )
    results = returned.reshape(item_count, channels, tokens) * out_scale
    mixed, gated_grad, filter_grad = (results[0], results[1], results[2])
    return (
        query_proj * mixed,
        out_cotangent * mixed,
        gated_grad * value_proj,
        gated_grad * key_proj,
        filter_grad,
    )


def halves(values):
    high = values.astype(jnp.bfloat16)
    return high, (values - high.astype(values.dtype)).astype(jnp.bfloat16)


def transform_tables(rows, scale):
    k1 = np.arange(rows)[:, None] * 2 + 1
    row_angle = -math.pi * ((k1 * np.arange(rows)[None, :]) % (4 * rows)) / (2 * rows)
    row_table = np.concatenate([np.cos(row_angle), np.sin(row_angle)])
    turn_period = 4 * rows * LANES
    turn_angle = -2.0 * math.pi * ((k1 * np.arange(LANES)[None, :]) % turn_period) / turn_period
    turn = np.concatenate([np.cos(turn_angle), np.sin(turn_angle)], axis=1).astype(np.float32)
    lane = np.arange(LANES)
    lane_angle = -2.0 * math.pi * ((lane[:, None] * lane[None, :]) % LANES) / LANES
    cos_lane, sin_lane = (np.cos(lane_angle), np.sin(lane_angle))
    lane_table = np.block([[cos_lane, sin_lane], [-sin_lane, cos_lane]])
    row_high, row_low = halves(row_table)
    back_high, back_low = halves(row_table.T * scale)
    lane_high, lane_low = halves(lane_table)
    return (
        np.concatenate([row_high, row_high, row_low], axis=1),
        turn,
        lane_high,
        lane_low,
        np.concatenate([back_high, back_high, back_low], axis=1),
    )


def pack_kernel(query_ref, key_ref, value_ref, taps_ref, cotangent_ref, out_ref, *, devices, share):
    runs = taps_ref.shape[1] // LANES
    stride = 3 * share * runs
    for c in range(share):
        for r in range(runs):
            at = (pl.ds(c * devices, devices), pl.ds(r * LANES, LANES))
            slabs = (
                key_ref[at] * value_ref[at],
                taps_ref[at],
                cotangent_ref[at] * query_ref[at],
            )
            for a, slab in enumerate(slabs):
                out_ref[pl.ds((a * share + c) * runs + r, devices, stride=stride), :] = slab


def unpack_kernel(
    packed_ref, query_ref, key_ref, value_ref, cotangent_ref,
    out_ref, query_grad_ref, key_grad_ref, value_grad_ref, taps_grad_ref, *, devices, share
):
    runs = query_ref.shape[1] // LANES
    stride = 3 * share * runs
    for c in range(share):
        for r in range(runs):
            at = (pl.ds(c * devices, devices), pl.ds(r * LANES, LANES))
            mixed, gated_grad, taps_grad = (
                packed_ref[pl.ds((a * share + c) * runs + r, devices, stride=stride), :] for a in range(3)
            )
            out_ref[at] = query_ref[at] * mixed
            query_grad_ref[at] = cotangent_ref[at] * mixed
            key_grad_ref[at] = gated_grad * value_ref[at]
            value_grad_ref[at] = gated_grad * key_ref[at]
            taps_grad_ref[at] = taps_grad


def dot(left, right, right_dim=0):
    return lax.dot_general(
        left, right, (((1,), (right_dim,)), ((), ())), preferred_element_type=jnp.float32
    )


def channels_kernel(
    packed_ref, row_ref, turn_ref, lane_high_ref, lane_low_ref, back_ref, out_ref, *, devices, share
):
    items = 3 * share
    runs = packed_ref.shape[0] // (devices * items)
    rows = runs * devices

    def columns(values):
        high, low = halves(values)
        return jnp.concatenate([high, low, high], axis=0)

    def along_lanes(values, right_dim):
        high, low = halves(values)
        lane_high = lane_high_ref[...]
        return (
            dot(high, lane_high, right_dim)
            + dot(low, lane_high, right_dim)
            + dot(high, lane_low_ref[...], right_dim)
        )

    turn_real = turn_ref[:, :LANES]
    turn_imag = turn_ref[:, LANES:]
    sequences = jnp.concatenate(
        [
            jnp.concatenate(
                [packed_ref[pl.ds((s * items + n) * runs, runs), :] for s in range(devices)], axis=0
            )
            for n in range(items)
        ],
        axis=1,
    )
    first = dot(row_ref[...], columns(sequences))
    turned = []
    for n in range(items):
        real = first[:rows, n * LANES : (n + 1) * LANES]
        imag = first[rows:, n * LANES : (n + 1) * LANES]
        turned.append(
            jnp.concatenate(
                [real * turn_real - imag * turn_imag, real * turn_imag + imag * turn_real], axis=1
            )
        )
    spectra = along_lanes(jnp.concatenate(turned, axis=0), 0)
    size = share * rows
    gated, taps, weighted = (
        (spectra[a * size : (a + 1) * size, :LANES], spectra[a * size : (a + 1) * size, LANES:])
        for a in range(3)
    )

    def product(left, right):
        return jnp.concatenate(
            [left[0] * right[0] - left[1] * right[1], left[0] * right[1] + left[1] * right[0]], axis=1
        )

    def against(left, right):
        return jnp.concatenate(
            [left[0] * right[0] + left[1] * right[1], left[0] * right[1] - left[1] * right[0]], axis=1
        )

    spectra = jnp.concatenate(
        [product(taps, gated), against(taps, weighted), against(gated, weighted)], axis=0
    )
    bins = along_lanes(spectra, 1)
    turned = []
    for n in range(items):
        real = bins[n * rows : (n + 1) * rows, :LANES]
        imag = bins[n * rows : (n + 1) * rows, LANES:]
        turned.append(
            jnp.concatenate(
                [real * turn_real + imag * turn_imag, imag * turn_real - real * turn_imag], axis=0
            )
        )
    results = dot(back_ref[...], columns(jnp.concatenate(turned, axis=1)))
    for n in range(items):
        for s in range(devices):
            out_ref[pl.ds((s * items + n) * runs, runs), :] = results[
                s * runs : (s + 1) * runs, n * LANES : (n + 1) * LANES
            ]


def in_vmem(count):
    return [pl.BlockSpec(memory_space=pltpu.VMEM)] * count


def channels_on_devices(query_proj, key_proj, value_proj, filter_taps, out_cotangent):
    devices = lax.axis_size("seq")
    channels, tokens = filter_taps.shape
    share = channels // devices
    rows = tokens * devices // LANES
    full_len = tokens * devices
    scale = 1.0 / (full_len * math.sqrt(full_len))
    packed_shape = jax.ShapeDtypeStruct((channels * 3 * tokens // LANES, LANES), jnp.float32)
    sizes = {"devices": devices, "share": share}

    def call(kernel, outs, *operands):
        many = isinstance(outs, list)
        return pl.pallas_call(
            lambda *refs: kernel(*refs, **sizes),
            name=kernel.__name__,
            out_shape=outs,
            in_specs=in_vmem(len(operands)),
            out_specs=in_vmem(len(outs)) if many else in_vmem(1)[0],
        )(*operands)

    def exchange(packed):
        blocks = packed.reshape(devices, -1, LANES)
        return lax.all_to_all(blocks, "seq", split_axis=0, concat_axis=0, tiled=True).reshape(packed.shape)

    packed = call(pack_kernel, packed_shape, query_proj, key_proj, value_proj, filter_taps, out_cotangent)
    tables = [jnp.asarray(table) for table in transform_tables(rows, scale)]
    results = call(channels_kernel, packed_shape, exchange(packed), *tables)
    outs = [jax.ShapeDtypeStruct((channels, tokens), jnp.float32)] * 5
    return tuple(
        call(unpack_kernel, outs, exchange(results), query_proj, key_proj, value_proj, out_cotangent)
    )


def per_device(query_proj, key_proj, value_proj, filter_taps, out_cotangent):
    devices = lax.axis_size("seq")
    channels, tokens = filter_taps.shape
    owns_channels = channels % devices == 0 and devices % SUBLANES == 0 and tokens % (LANES * SUBLANES) == 0
    plan = channels_on_devices if owns_channels else bins_over_devices
    return plan(query_proj, key_proj, value_proj, filter_taps, out_cotangent)


def solution(mesh):
    placed = (P("ch", "seq"), P("ch", "seq"), P("ch", "seq"), P("ch", "seq"), P("ch", "seq"))
    return jax.shard_map(
        per_device,
        mesh=mesh,
        in_specs=placed,
        out_specs=(P("ch", "seq"), P("ch", "seq"), P("ch", "seq"), P("ch", "seq"), P("ch", "seq")),
        check_vma=False,
    )
```

profile of v0, /device:TPU:0, one launch (start us, length us, event | category | flops | bytes accessed | tf_op | source)
XLA Modules:
  0.0 34.3 jit_solution(17708553416435829483)
XLA Ops:
  0.6 1.7 %pack_kernel.1 = f32[384,128]{1,0:T(8,128)} custom-call(f32[16,1024]{1,0:T(8,128)} %refs_1_.4, f32[16,1024]{1,0:T(8,128)} %refs_2_.4, f32[16,1024]{1,0:T(8,128)} %refs_3_.4, f32[16,1024]{1,0:T(8,128)} %refs_3_.3, f32[16,1024]{1,0:T(8,128)} %refs_4_.4), custom_call_target="tpu_custom_call" | custom-call | tf_op jit(solution)/shard_map/pack_kernel/pallas_call | solution.py:306
  2.3 15.4 %all_to_all.10 = f32[8,48,128]{2,1,0:T(8,128)} all-to-all(f32[8,48,128]{2,1,0:T(8,128)} %bitcast.7), channel_id=1, replica_groups=mesh['seq'=8,'ch'=4] {'seq'}, dimensions={0} | all-to-all | bytes 393216 | tf_op jit(solution)/shard_map/all_to_all | solution.py:316
  17.7 3.0 %channels_kernel.1 = f32[384,128]{1,0:T(8,128)} custom-call(f32[384,128]{1,0:T(8,128)} %bitcast.5, bf16[128,192]{1,0:T(8,128)(2,1)} %constant.10.clone.refs_1_, f32[64,256]{1,0:T(8,128)} %constant.11.clone.refs_2_, bf16[256,256]{1,0:T(8,128)(2,1)} %constant.12.clone.refs_3_, bf16[256,256]{1,0:T(8,128)(2,1)} %constant.13.clone.refs_4_, ...), custom_call_target="tpu_custom_call" | custom-call | tf_op jit(solution)/shard_map/channels_kernel/pallas_call | solution.py:306
  20.7 11.8 %all_to_all.11 = f32[8,48,128]{2,1,0:T(8,128)} all-to-all(f32[8,48,128]{2,1,0:T(8,128)} %bitcast.6), channel_id=1, replica_groups=mesh['seq'=8,'ch'=4] {'seq'}, dimensions={0} | all-to-all | bytes 393216 | tf_op jit(solution)/shard_map/all_to_all | solution.py:316
  32.5 1.8 %unpack_kernel.1 = (f32[16,1024]{1,0:T(8,128)}, f32[16,1024]{1,0:T(8,128)}, f32[16,1024]{1,0:T(8,128)}, f32[16,1024]{1,0:T(8,128)}, f32[16,1024]{1,0:T(8,128)}) custom-call(f32[384,128]{1,0:T(8,128)} %bitcast.4, f32[16,1024]{1,0:T(8,128)} %refs_1_.4, f32[16,1024]{1,0:T(8,128)} %refs_2_.4, f32[16,1024]{1,0:T(8,128)} %refs_3_.4, f32[16,1024]{1,0:T(8,128)} %refs_4_.4), custom_call_target="tpu_custom_call" | custom-call | tf_op jit(solution)/shard_map/unpack_kernel/pallas_call | solution.py:306
where the time goes:
time: 34.7 us; the launch traced here: 34.3 us
  blocking collectives  27.1 us (78%)
  Pallas kernels  6.48 us (19%)
  between operations  0.63 us (2%)
    all_to_all x2, blocking collectives, exchange(): lax.all_to_all(blocks, 'seq', split_axis=0, concat_axis=0, tiled=True)  27.1 us
    pallas_call x3, Pallas kernels, call(): pl.pallas_call(lambda *refs: kernel(*refs, **sizes), name=kernel.__name__...  6.48 us

commit v1 on v0

--- a/solution.py
+++ b/solution.py
@@ -11,6 +11,7 @@
 FAC = 512
 LANES = 128
 SUBLANES = 8
+KERNEL_VMEM = 16 * 2**20
 
 
 exact_mode = lax.Precision.HIGHEST
@@ -168,7 +169,26 @@
     )
 
 
-def pack_kernel(query_ref, key_ref, value_ref, taps_ref, cotangent_ref, out_ref, *, devices, share):
+def pack_kernel(
+    query_hbm, key_hbm, value_hbm, taps_hbm, cotangent_hbm, out_ref,
+    query_ref, key_ref, value_ref, taps_ref, cotangent_ref, arrived, *, devices, share
+):
+    copies = [
+        pltpu.make_async_copy(source, target, arrived.at[i])
+        for i, (source, target) in enumerate(
+            (
+                (query_hbm, query_ref),
+                (key_hbm, key_ref),
+                (value_hbm, value_ref),
+                (taps_hbm, taps_ref),
+                (cotangent_hbm, cotangent_ref),
+            )
+        )
+    ]
+    for copy in copies:
+        copy.start()
+    for copy in copies:
+        copy.wait()
     runs = taps_ref.shape[1] // LANES
     stride = 3 * share * runs
     for c in range(share):
@@ -301,21 +321,29 @@
     packed_shape = jax.ShapeDtypeStruct((channels * 3 * tokens // LANES, LANES), jnp.float32)
     sizes = {"devices": devices, "share": share}
 
-    def call(kernel, outs, *operands):
+    def call(kernel, outs, *operands, space=pltpu.VMEM, scratch=()):
         many = isinstance(outs, list)
         return pl.pallas_call(
             lambda *refs: kernel(*refs, **sizes),
             name=kernel.__name__,
+            compiler_params=pltpu.CompilerParams(vmem_limit_bytes=KERNEL_VMEM),
             out_shape=outs,
-            in_specs=in_vmem(len(operands)),
+            in_specs=[pl.BlockSpec(memory_space=space)] * len(operands),
             out_specs=in_vmem(len(outs)) if many else in_vmem(1)[0],
+            scratch_shapes=scratch,
         )(*operands)
 
     def exchange(packed):
         blocks = packed.reshape(devices, -1, LANES)
         return lax.all_to_all(blocks, "seq", split_axis=0, concat_axis=0, tiled=True).reshape(packed.shape)
 
-    packed = call(pack_kernel, packed_shape, query_proj, key_proj, value_proj, filter_taps, out_cotangent)
+    inputs = [
+        pltpu.with_memory_space_constraint(x, pltpu.HBM)
+        for x in (query_proj, key_proj, value_proj, filter_taps, out_cotangent)
+    ]
+    landing = [pltpu.VMEM((channels, tokens), jnp.float32) for _ in inputs]
+    landing.append(pltpu.SemaphoreType.DMA((len(inputs),)))
+    packed = call(pack_kernel, packed_shape, *inputs, space=pltpu.HBM, scratch=landing)
     tables = [jnp.asarray(table) for table in transform_tables(rows, scale)]
     results = call(channels_kernel, packed_shape, exchange(packed), *tables)
     outs = [jax.ShapeDtypeStruct((channels, tokens), jnp.float32)] * 5

time: 34.7 us -> 30.2 us (0.87)
  Pallas kernels: 6.48 us -> 3.04 us
  blocking collectives: 27.1 us -> 26.1 us
    pallas_call x3, Pallas kernels: 6.48 us -> 3.04 us  [call(): pl.pallas_call(lambda *refs: kernel(*refs, **sizes), name=kernel.__name__...]
    all_to_all x2, blocking collectives: 27.1 us -> 26.1 us  [exchange(): lax.all_to_all(blocks, 'seq', split_axis=0, concat_axis=0, tiled=True)]
where the time goes in v1:
time: 30.2 us; the launch traced here: 29.9 us
  blocking collectives  26.1 us (86%)
  Pallas kernels  3.04 us (10%)
  between operations  0.75 us (2%)
    all_to_all x2, blocking collectives, exchange(): lax.all_to_all(blocks, 'seq', split_axis=0, concat_axis=0, tiled=True)  26.1 us
    pallas_call x3, Pallas kernels, call(): pl.pallas_call(lambda *refs: kernel(*refs, **sizes), name=kernel.__name__...  3.04 us

profile of v1, /device:TPU:0, one launch (start us, length us, event | category | flops | bytes accessed | tf_op | source)
XLA Modules:
  0.0 29.9 jit_solution(12977257993797704052)
XLA Ops:
  0.6 0.0 copy-start.8
  0.6 1.1 %pack_kernel.1 = f32[384,128]{1,0:T(8,128)S(1)} custom-call(f32[16,1024]{1,0:T(8,128)} %refs_1_.4, f32[16,1024]{1,0:T(8,128)} %refs_2_.4, f32[16,1024]{1,0:T(8,128)} %refs_3_.4, f32[16,1024]{1,0:T(8,128)} %refs_3_.3, f32[16,1024]{1,0:T(8,128)} %refs_4_.4), custom_call_target="tpu_custom_call" | custom-call | tf_op jit(solution)/shard_map/pack_kernel/pallas_call | solution.py:326
  1.7 0.0 copy-start.4
  1.8 0.0 copy-start.5
  1.8 0.0 copy-start.6
  1.8 0.0 copy-start.7
  1.8 15.2 %all_to_all.10 = f32[8,48,128]{2,1,0:T(8,128)S(1)} all-to-all(f32[8,48,128]{2,1,0:T(8,128)S(1)} %bitcast.7), channel_id=1, replica_groups=mesh['seq'=8,'ch'=4] {'seq'}, dimensions={0} | all-to-all | bytes 393216 | tf_op jit(solution)/shard_map/all_to_all | solution.py:338
  17.0 0.0 copy-done.8
  17.0 0.0 copy-done.4
  17.0 0.0 copy-done.5
  17.0 0.0 copy-done.6
  17.0 0.0 copy-done.7
  17.0 1.2 %channels_kernel.1 = f32[384,128]{1,0:T(8,128)S(1)} custom-call(f32[384,128]{1,0:T(8,128)S(1)} %bitcast.5, bf16[128,192]{1,0:T(8,128)(2,1)S(1)} %copy-done.7, f32[64,256]{1,0:T(8,128)S(1)} %copy-done.6, bf16[256,256]{1,0:T(8,128)(2,1)S(1)} %copy-done.5, bf16[256,256]{1,0:T(8,128)(2,1)S(1)} %copy-done.4, bf16[64,384]{1,0:T(8,128)(2,1)S(1)} %copy-done.8), custom_call_target="tpu_custom_call" | custom-call | tf_op jit(solution)/shard_map/channels_kernel/pallas_call | solution.py:326
  18.2 0.0 copy-start
  18.2 0.0 copy-start.1
  18.2 0.0 copy-start.2
  18.2 0.0 copy-start.3
  18.2 10.9 %all_to_all.11 = f32[8,48,128]{2,1,0:T(8,128)S(1)} all-to-all(f32[8,48,128]{2,1,0:T(8,128)S(1)} %bitcast.6), channel_id=1, replica_groups=mesh['seq'=8,'ch'=4] {'seq'}, dimensions={0} | all-to-all | bytes 393216 | tf_op jit(solution)/shard_map/all_to_all | solution.py:338
  29.1 0.0 copy-done
  29.1 0.0 copy-done.1
  29.1 0.0 copy-done.2
  29.1 0.0 copy-done.3
  29.1 0.8 %unpack_kernel.1 = (f32[16,1024]{1,0:T(8,128)}, f32[16,1024]{1,0:T(8,128)}, f32[16,1024]{1,0:T(8,128)}, f32[16,1024]{1,0:T(8,128)}, f32[16,1024]{1,0:T(8,128)}) custom-call(f32[384,128]{1,0:T(8,128)S(1)} %bitcast.4, f32[16,1024]{1,0:T(8,128)S(1)} %copy-done, f32[16,1024]{1,0:T(8,128)S(1)} %copy-done.1, f32[16,1024]{1,0:T(8,128)S(1)} %copy-done.2, ...), custom_call_target="tpu_custom_call" | custom-call | tf_op jit(solution)/shard_map/unpack_kernel/pallas_call | solution.py:326
Async XLA Ops:
  0.6 16.4 %copy-start.8 = (bf16[64,384]{1,0:T(8,128)(2,1)S(1)}, bf16[64,384]{1,0:T(8,128)(2,1)}, u32[]{:S(2)}) copy-start(bf16[64,384]{1,0:T(8,128)(2,1)} %constant.14.clone.refs_5_) | copy-start | bytes 147460
  1.7 15.2 %copy-start.4 = (bf16[256,256]{1,0:T(8,128)(2,1)S(1)}, bf16[256,256]{1,0:T(8,128)(2,1)}, u32[]{:S(2)}) copy-start(bf16[256,256]{1,0:T(8,128)(2,1)} %constant.13.clone.refs_4_) | copy-start | bytes 393220
  1.8 15.2 %copy-start.5 = (bf16[256,256]{1,0:T(8,128)(2,1)S(1)}, bf16[256,256]{1,0:T(8,128)(2,1)}, u32[]{:S(2)}) copy-start(bf16[256,256]{1,0:T(8,128)(2,1)} %constant.12.clone.refs_3_) | copy-start | bytes 393220
  1.8 15.2 %copy-start.6 = (f32[64,256]{1,0:T(8,128)S(1)}, f32[64,256]{1,0:T(8,128)}, u32[]{:S(2)}) copy-start(f32[64,256]{1,0:T(8,128)} %constant.11.clone.refs_2_) | copy-start | bytes 196612
  1.8 15.2 %copy-start.7 = (bf16[128,192]{1,0:T(8,128)(2,1)S(1)}, bf16[128,192]{1,0:T(8,128)(2,1)}, u32[]{:S(2)}) copy-start(bf16[128,192]{1,0:T(8,128)(2,1)} %constant.10.clone.refs_1_) | copy-start | bytes 147460
  18.2 10.9 %copy-start = (f32[16,1024]{1,0:T(8,128)S(1)}, f32[16,1024]{1,0:T(8,128)}, u32[]{:S(2)}) copy-start(f32[16,1024]{1,0:T(8,128)} %refs_1_.4) | copy-start | bytes 196612
  18.2 10.9 %copy-start.1 = (f32[16,1024]{1,0:T(8,128)S(1)}, f32[16,1024]{1,0:T(8,128)}, u32[]{:S(2)}) copy-start(f32[16,1024]{1,0:T(8,128)} %refs_2_.4) | copy-start | bytes 196612
  18.2 10.9 %copy-start.2 = (f32[16,1024]{1,0:T(8,128)S(1)}, f32[16,1024]{1,0:T(8,128)}, u32[]{:S(2)}) copy-start(f32[16,1024]{1,0:T(8,128)} %refs_3_.4) | copy-start | bytes 196612
  18.2 10.9 %copy-start.3 = (f32[16,1024]{1,0:T(8,128)S(1)}, f32[16,1024]{1,0:T(8,128)}, u32[]{:S(2)}) copy-start(f32[16,1024]{1,0:T(8,128)} %refs_4_.4) | copy-start | bytes 196612

commit v2 on v1

--- a/solution.py
+++ b/solution.py
@@ -169,6 +169,10 @@
     )
 
 
+def exchange_order(devices):
+    return [(devices // 2 + 1 - i) % devices for i in range(devices)]
+
+
 def pack_kernel(
     query_hbm, key_hbm, value_hbm, taps_hbm, cotangent_hbm, out_ref,
     query_ref, key_ref, value_ref, taps_ref, cotangent_ref, arrived, *, devices, share
@@ -232,6 +236,7 @@
     packed_ref, row_ref, turn_ref, lane_high_ref, lane_low_ref, back_ref, out_ref, *, devices, share
 ):
     items = 3 * share
+    order = exchange_order(devices)
     runs = packed_ref.shape[0] // (devices * items)
     rows = runs * devices
 
@@ -253,7 +258,8 @@
     sequences = jnp.concatenate(
         [
             jnp.concatenate(
-                [packed_ref[pl.ds((s * items + n) * runs, runs), :] for s in range(devices)], axis=0
+                [packed_ref[pl.ds((order.index(s) * items + n) * runs, runs), :] for s in range(devices)],
+                axis=0,
             )
             for n in range(items)
         ],
@@ -302,7 +308,7 @@
     results = dot(back_ref[...], columns(jnp.concatenate(turned, axis=1)))
     for n in range(items):
         for s in range(devices):
-            out_ref[pl.ds((s * items + n) * runs, runs), :] = results[
+            out_ref[pl.ds((order.index(s) * items + n) * runs, runs), :] = results[
                 s * runs : (s + 1) * runs, n * LANES : (n + 1) * LANES
             ]
 
@@ -335,7 +341,10 @@
 
     def exchange(packed):
         blocks = packed.reshape(devices, -1, LANES)
-        return lax.all_to_all(blocks, "seq", split_axis=0, concat_axis=0, tiled=True).reshape(packed.shape)
+        received = lax.all_to_all(
+            blocks, "seq", split_axis=0, concat_axis=0, tiled=True, axis_index_groups=[exchange_order(devices)]
+        )
+        return received.reshape(packed.shape)
 
     inputs = [
         pltpu.with_memory_space_constraint(x, pltpu.HBM)

time: 30.2 us -> 26 us (0.86)
  blocking collectives: 26.1 us -> 21.9 us
    all_to_all x2, blocking collectives: 26.1 us -> 21.9 us  [exchange(): lax.all_to_all(blocks, 'seq', split_axis=0, concat_axis=0, tiled=True, ax...]
where the time goes in v2:
time: 26 us; the launch traced here: 25.8 us
  blocking collectives  21.9 us (84%)
  Pallas kernels  3.04 us (12%)
  between operations  0.75 us (3%)
    all_to_all x2, blocking collectives, exchange(): lax.all_to_all(blocks, 'seq', split_axis=0, concat_axis=0, tiled=True, ax...  21.9 us
    pallas_call x3, Pallas kernels, call(): pl.pallas_call(lambda *refs: kernel(*refs, **sizes), name=kernel.__name__...  3.04 us

profile of v2, /device:TPU:0, one launch (start us, length us, event | category | flops | bytes accessed | tf_op | source)
XLA Modules:
  0.0 25.8 jit_solution(16558403765726796985)
XLA Ops:
  0.6 0.0 copy-start.8
  0.6 1.1 %pack_kernel.1 = f32[384,128]{1,0:T(8,128)S(1)} custom-call(f32[16,1024]{1,0:T(8,128)} %refs_1_.4, f32[16,1024]{1,0:T(8,128)} %refs_2_.4, f32[16,1024]{1,0:T(8,128)} %refs_3_.4, f32[16,1024]{1,0:T(8,128)} %refs_3_.3, f32[16,1024]{1,0:T(8,128)} %refs_4_.4), custom_call_target="tpu_custom_call" | custom-call | tf_op jit(solution)/shard_map/pack_kernel/pallas_call | solution.py:332
  1.7 0.0 copy-start.4
  1.8 0.0 copy-start.5
  1.8 0.0 copy-start.6
  1.8 0.0 copy-start.7
  1.8 12.9 %all_to_all.10 = f32[8,48,128]{2,1,0:T(8,128)S(1)} all-to-all(f32[8,48,128]{2,1,0:T(8,128)S(1)} %bitcast.7), channel_id=1, replica_groups={{20,16,12,8,4,0,28,24},{21,17,13,9,5,1,29,25},{22,18,14,10,6,2,30,26},{..., dimensions={0} | all-to-all | bytes 393216 | tf_op jit(solution)/shard_map/all_to_all | solution.py:344
  14.7 0.0 copy-done.8
  14.7 0.0 copy-done.4
  14.7 0.0 copy-done.5
  14.7 0.0 copy-done.6
  14.7 0.0 copy-done.7
  14.7 1.2 %channels_kernel.1 = f32[384,128]{1,0:T(8,128)S(1)} custom-call(f32[384,128]{1,0:T(8,128)S(1)} %bitcast.5, bf16[128,192]{1,0:T(8,128)(2,1)S(1)} %copy-done.7, f32[64,256]{1,0:T(8,128)S(1)} %copy-done.6, bf16[256,256]{1,0:T(8,128)(2,1)S(1)} %copy-done.5, bf16[256,256]{1,0:T(8,128)(2,1)S(1)} %copy-done.4, bf16[64,384]{1,0:T(8,128)(2,1)S(1)} %copy-done.8), custom_call_target="tpu_custom_call" | custom-call | tf_op jit(solution)/shard_map/channels_kernel/pallas_call | solution.py:332
  15.9 0.0 copy-start
  15.9 0.0 copy-start.1
  15.9 0.0 copy-start.2
  15.9 0.0 copy-start.3
  16.0 9.0 %all_to_all.11 = f32[8,48,128]{2,1,0:T(8,128)S(1)} all-to-all(f32[8,48,128]{2,1,0:T(8,128)S(1)} %bitcast.6), channel_id=1, replica_groups={{20,16,12,8,4,0,28,24},{21,17,13,9,5,1,29,25},{22,18,14,10,6,2,30,26},{..., dimensions={0} | all-to-all | bytes 393216 | tf_op jit(solution)/shard_map/all_to_all | solution.py:344
  25.0 0.0 copy-done
  25.0 0.0 copy-done.1
  25.0 0.0 copy-done.2
  25.0 0.0 copy-done.3
  25.0 0.8 %unpack_kernel.1 = (f32[16,1024]{1,0:T(8,128)}, f32[16,1024]{1,0:T(8,128)}, f32[16,1024]{1,0:T(8,128)}, f32[16,1024]{1,0:T(8,128)}, f32[16,1024]{1,0:T(8,128)}) custom-call(f32[384,128]{1,0:T(8,128)S(1)} %bitcast.4, f32[16,1024]{1,0:T(8,128)S(1)} %copy-done, f32[16,1024]{1,0:T(8,128)S(1)} %copy-done.1, f32[16,1024]{1,0:T(8,128)S(1)} %copy-done.2, ...), custom_call_target="tpu_custom_call" | custom-call | tf_op jit(solution)/shard_map/unpack_kernel/pallas_call | solution.py:332
Async XLA Ops:
  0.6 14.1 %copy-start.8 = (bf16[64,384]{1,0:T(8,128)(2,1)S(1)}, bf16[64,384]{1,0:T(8,128)(2,1)}, u32[]{:S(2)}) copy-start(bf16[64,384]{1,0:T(8,128)(2,1)} %constant.14.clone.refs_5_) | copy-start | bytes 147460
  1.7 13.0 %copy-start.4 = (bf16[256,256]{1,0:T(8,128)(2,1)S(1)}, bf16[256,256]{1,0:T(8,128)(2,1)}, u32[]{:S(2)}) copy-start(bf16[256,256]{1,0:T(8,128)(2,1)} %constant.13.clone.refs_4_) | copy-start | bytes 393220
  1.8 13.0 %copy-start.5 = (bf16[256,256]{1,0:T(8,128)(2,1)S(1)}, bf16[256,256]{1,0:T(8,128)(2,1)}, u32[]{:S(2)}) copy-start(bf16[256,256]{1,0:T(8,128)(2,1)} %constant.12.clone.refs_3_) | copy-start | bytes 393220
  1.8 13.0 %copy-start.6 = (f32[64,256]{1,0:T(8,128)S(1)}, f32[64,256]{1,0:T(8,128)}, u32[]{:S(2)}) copy-start(f32[64,256]{1,0:T(8,128)} %constant.11.clone.refs_2_) | copy-start | bytes 196612
  1.8 13.0 %copy-start.7 = (bf16[128,192]{1,0:T(8,128)(2,1)S(1)}, bf16[128,192]{1,0:T(8,128)(2,1)}, u32[]{:S(2)}) copy-start(bf16[128,192]{1,0:T(8,128)(2,1)} %constant.10.clone.refs_1_) | copy-start | bytes 147460
  15.9 9.0 %copy-start = (f32[16,1024]{1,0:T(8,128)S(1)}, f32[16,1024]{1,0:T(8,128)}, u32[]{:S(2)}) copy-start(f32[16,1024]{1,0:T(8,128)} %refs_1_.4) | copy-start | bytes 196612
  15.9 9.0 %copy-start.1 = (f32[16,1024]{1,0:T(8,128)S(1)}, f32[16,1024]{1,0:T(8,128)}, u32[]{:S(2)}) copy-start(f32[16,1024]{1,0:T(8,128)} %refs_2_.4) | copy-start | bytes 196612
  15.9 9.0 %copy-start.2 = (f32[16,1024]{1,0:T(8,128)S(1)}, f32[16,1024]{1,0:T(8,128)}, u32[]{:S(2)}) copy-start(f32[16,1024]{1,0:T(8,128)} %refs_3_.4) | copy-start | bytes 196612
  15.9 9.0 %copy-start.3 = (f32[16,1024]{1,0:T(8,128)S(1)}, f32[16,1024]{1,0:T(8,128)}, u32[]{:S(2)}) copy-start(f32[16,1024]{1,0:T(8,128)} %refs_4_.4) | copy-start | bytes 196612

commit v3 on v2

--- a/solution.py
+++ b/solution.py
@@ -165,37 +165,45 @@
         turn,
         lane_high,
         lane_low,
-        np.concatenate([back_high, back_high, back_low], axis=1),
+        np.concatenate(
+            [np.concatenate([back_high, back_high], axis=1), np.concatenate([back_low, np.zeros_like(back_low)], axis=1)]
+        ),
     )
 
 
 def exchange_order(devices):
-    return [(devices // 2 + 1 - i) % devices for i in range(devices)]
+    middle = devices // 2 + 1
+    order = list(range(middle, -1, -1))
+    above = list(range(devices - 1, middle, -1))
+    step = len(order) // max(len(above), 1)
+    for i, device in enumerate(above):
+        order.insert((i + 1) * step + i, device)
+    return order
 
 
 def pack_kernel(
     query_hbm, key_hbm, value_hbm, taps_hbm, cotangent_hbm, out_ref,
     query_ref, key_ref, value_ref, taps_ref, cotangent_ref, arrived, *, devices, share
 ):
+    sources = (query_hbm, key_hbm, value_hbm, taps_hbm, cotangent_hbm)
+    targets = (query_ref, key_ref, value_ref, taps_ref, cotangent_ref)
     copies = [
-        pltpu.make_async_copy(source, target, arrived.at[i])
-        for i, (source, target) in enumerate(
-            (
-                (query_hbm, query_ref),
-                (key_hbm, key_ref),
-                (value_hbm, value_ref),
-                (taps_hbm, taps_ref),
-                (cotangent_hbm, cotangent_ref),
-            )
-        )
+        [
+            pltpu.make_async_copy(
+                source.at[pl.ds(c * devices, devices)], target.at[pl.ds(c * devices, devices)], arrived.at[c, i]
+            )
+            for i, (source, target) in enumerate(zip(sources, targets))
+        ]
+        for c in range(share)
     ]
-    for copy in copies:
-        copy.start()
-    for copy in copies:
-        copy.wait()
+    for group in copies:
+        for copy in group:
+            copy.start()
     runs = taps_ref.shape[1] // LANES
     stride = 3 * share * runs
     for c in range(share):
+        for copy in copies[c]:
+            copy.wait()
         for r in range(runs):
             at = (pl.ds(c * devices, devices), pl.ds(r * LANES, LANES))
             slabs = (
@@ -246,12 +254,9 @@
 
     def along_lanes(values, right_dim):
         high, low = halves(values)
-        lane_high = lane_high_ref[...]
-        return (
-            dot(high, lane_high, right_dim)
-            + dot(low, lane_high, right_dim)
-            + dot(high, lane_low_ref[...], right_dim)
-        )
+        size = values.shape[0]
+        both = dot(jnp.concatenate([high, low], axis=0), lane_high_ref[...], right_dim)
+        return both[:size] + both[size:] + dot(high, lane_low_ref[...], right_dim)
 
     turn_real = turn_ref[:, :LANES]
     turn_imag = turn_ref[:, LANES:]
@@ -305,7 +310,9 @@
                 [real * turn_real + imag * turn_imag, imag * turn_real - real * turn_imag], axis=0
             )
         )
-    results = dot(back_ref[...], columns(jnp.concatenate(turned, axis=1)))
+    high, low = halves(jnp.concatenate(turned, axis=1))
+    both = dot(back_ref[...], jnp.concatenate([high, low], axis=0))
+    results = both[:rows] + both[rows:]
     for n in range(items):
         for s in range(devices):
             out_ref[pl.ds((order.index(s) * items + n) * runs, runs), :] = results[
@@ -351,7 +358,7 @@
         for x in (query_proj, key_proj, value_proj, filter_taps, out_cotangent)
     ]
     landing = [pltpu.VMEM((channels, tokens), jnp.float32) for _ in inputs]
-    landing.append(pltpu.SemaphoreType.DMA((len(inputs),)))
+    landing.append(pltpu.SemaphoreType.DMA((share, len(inputs))))
     packed = call(pack_kernel, packed_shape, *inputs, space=pltpu.HBM, scratch=landing)
     tables = [jnp.asarray(table) for table in transform_tables(rows, scale)]
     results = call(channels_kernel, packed_shape, exchange(packed), *tables)

time: 26 us -> 25.7 us (0.988)
  no operation moved by 1% of the time
where the time goes in v3:
time: 25.7 us; the launch traced here: 25.5 us
  blocking collectives  21.7 us (84%)
  Pallas kernels  2.97 us (12%)
  between operations  0.75 us (3%)
    all_to_all x2, blocking collectives, exchange(): lax.all_to_all(blocks, 'seq', split_axis=0, concat_axis=0, tiled=True, ax...  21.7 us
    pallas_call x3, Pallas kernels, call(): pl.pallas_call(lambda *refs: kernel(*refs, **sizes), name=kernel.__name__...  2.97 us

profile of v3, /device:TPU:0, one launch (start us, length us, event | category | flops | bytes accessed | tf_op | source)
XLA Modules:
  0.0 25.5 jit_solution(16276536438122073422)
XLA Ops:
  0.6 0.0 copy-start.8
  0.6 1.1 %pack_kernel.1 = f32[384,128]{1,0:T(8,128)S(1)} custom-call(f32[16,1024]{1,0:T(8,128)} %refs_1_.4, f32[16,1024]{1,0:T(8,128)} %refs_2_.4, f32[16,1024]{1,0:T(8,128)} %refs_3_.4, f32[16,1024]{1,0:T(8,128)} %refs_3_.3, f32[16,1024]{1,0:T(8,128)} %refs_4_.4), custom_call_target="tpu_custom_call" | custom-call | tf_op jit(solution)/shard_map/pack_kernel/pallas_call | solution.py:339
  1.7 0.0 copy-start.4
  1.7 0.0 copy-start.5
  1.7 0.0 copy-start.6
  1.7 0.0 copy-start.7
  1.8 12.1 %all_to_all.10 = f32[8,48,128]{2,1,0:T(8,128)S(1)} all-to-all(f32[8,48,128]{2,1,0:T(8,128)S(1)} %bitcast.5), channel_id=1, replica_groups={{20,16,12,28,8,4,0,24},{21,17,13,29,9,5,1,25},{22,18,14,30,10,6,2,26},{..., dimensions={0} | all-to-all | bytes 393216 | tf_op jit(solution)/shard_map/all_to_all | solution.py:351
  13.9 0.0 copy-done.8
  13.9 0.0 copy-done.4
  13.9 0.0 copy-done.5
  13.9 0.0 copy-done.6
  13.9 0.0 copy-done.7
  13.9 1.1 %channels_kernel.1 = f32[384,128]{1,0:T(8,128)S(1)} custom-call(f32[384,128]{1,0:T(8,128)S(1)} %bitcast.6, bf16[128,192]{1,0:T(8,128)(2,1)S(1)} %copy-done.8, f32[64,256]{1,0:T(8,128)S(1)} %copy-done.7, bf16[256,256]{1,0:T(8,128)(2,1)S(1)} %copy-done.5, bf16[256,256]{1,0:T(8,128)(2,1)S(1)} %copy-done.4, bf16[128,256]{1,0:T(8,128)(2,1)S(1)} %copy-done.6), custom_call_target="tpu_custom_call" | custom-call | tf_op jit(solution)/shard_map/channels_kernel/pallas_call | solution.py:339
  15.1 0.0 copy-start
  15.1 0.0 copy-start.1
  15.1 0.0 copy-start.2
  15.1 0.0 copy-start.3
  15.1 9.6 %all_to_all.11 = f32[8,48,128]{2,1,0:T(8,128)S(1)} all-to-all(f32[8,48,128]{2,1,0:T(8,128)S(1)} %bitcast.7), channel_id=1, replica_groups={{20,16,12,28,8,4,0,24},{21,17,13,29,9,5,1,25},{22,18,14,30,10,6,2,26},{..., dimensions={0} | all-to-all | bytes 393216 | tf_op jit(solution)/shard_map/all_to_all | solution.py:351
  24.7 0.0 copy-done
  24.7 0.0 copy-done.1
  24.7 0.0 copy-done.2
  24.7 0.0 copy-done.3
  24.7 0.8 %unpack_kernel.1 = (f32[16,1024]{1,0:T(8,128)}, f32[16,1024]{1,0:T(8,128)}, f32[16,1024]{1,0:T(8,128)}, f32[16,1024]{1,0:T(8,128)}, f32[16,1024]{1,0:T(8,128)}) custom-call(f32[384,128]{1,0:T(8,128)S(1)} %bitcast.4, f32[16,1024]{1,0:T(8,128)S(1)} %copy-done, f32[16,1024]{1,0:T(8,128)S(1)} %copy-done.1, f32[16,1024]{1,0:T(8,128)S(1)} %copy-done.2, ...), custom_call_target="tpu_custom_call" | custom-call | tf_op jit(solution)/shard_map/unpack_kernel/pallas_call | solution.py:339
Async XLA Ops:
  0.6 13.3 %copy-start.8 = (bf16[128,192]{1,0:T(8,128)(2,1)S(1)}, bf16[128,192]{1,0:T(8,128)(2,1)}, u32[]{:S(2)}) copy-start(bf16[128,192]{1,0:T(8,128)(2,1)} %constant.10.clone.refs_1_) | copy-start | bytes 147460
  1.7 12.2 %copy-start.4 = (bf16[256,256]{1,0:T(8,128)(2,1)S(1)}, bf16[256,256]{1,0:T(8,128)(2,1)}, u32[]{:S(2)}) copy-start(bf16[256,256]{1,0:T(8,128)(2,1)} %constant.13.clone.refs_4_) | copy-start | bytes 393220
  1.7 12.2 %copy-start.5 = (bf16[256,256]{1,0:T(8,128)(2,1)S(1)}, bf16[256,256]{1,0:T(8,128)(2,1)}, u32[]{:S(2)}) copy-start(bf16[256,256]{1,0:T(8,128)(2,1)} %constant.12.clone.refs_3_) | copy-start | bytes 393220
  1.7 12.2 %copy-start.6 = (bf16[128,256]{1,0:T(8,128)(2,1)S(1)}, bf16[128,256]{1,0:T(8,128)(2,1)}, u32[]{:S(2)}) copy-start(bf16[128,256]{1,0:T(8,128)(2,1)} %constant.14.clone.refs_5_) | copy-start | bytes 196612
  1.7 12.2 %copy-start.7 = (f32[64,256]{1,0:T(8,128)S(1)}, f32[64,256]{1,0:T(8,128)}, u32[]{:S(2)}) copy-start(f32[64,256]{1,0:T(8,128)} %constant.11.clone.refs_2_) | copy-start | bytes 196612
  15.1 9.6 %copy-start = (f32[16,1024]{1,0:T(8,128)S(1)}, f32[16,1024]{1,0:T(8,128)}, u32[]{:S(2)}) copy-start(f32[16,1024]{1,0:T(8,128)} %refs_1_.4) | copy-start | bytes 196612
  15.1 9.6 %copy-start.1 = (f32[16,1024]{1,0:T(8,128)S(1)}, f32[16,1024]{1,0:T(8,128)}, u32[]{:S(2)}) copy-start(f32[16,1024]{1,0:T(8,128)} %refs_2_.4) | copy-start | bytes 196612
  15.1 9.6 %copy-start.2 = (f32[16,1024]{1,0:T(8,128)S(1)}, f32[16,1024]{1,0:T(8,128)}, u32[]{:S(2)}) copy-start(f32[16,1024]{1,0:T(8,128)} %refs_3_.4) | copy-start | bytes 196612
  15.1 9.6 %copy-start.3 = (f32[16,1024]{1,0:T(8,128)S(1)}, f32[16,1024]{1,0:T(8,128)}, u32[]{:S(2)}) copy-start(f32[16,1024]{1,0:T(8,128)} %refs_4_.4) | copy-start | bytes 196612

commit v4 on v3

--- a/solution.py
+++ b/solution.py
@@ -172,7 +172,7 @@
 
 
 def exchange_order(devices):
-    middle = devices // 2 + 1
+    middle = min(devices // 2 + 1, devices - 1)
     order = list(range(middle, -1, -1))
     above = list(range(devices - 1, middle, -1))
     step = len(order) // max(len(above), 1)
@@ -182,8 +182,8 @@
 
 
 def pack_kernel(
-    query_hbm, key_hbm, value_hbm, taps_hbm, cotangent_hbm, out_ref,
-    query_ref, key_ref, value_ref, taps_ref, cotangent_ref, arrived, *, devices, share
+    query_hbm, key_hbm, value_hbm, taps_hbm, cotangent_hbm,
+    packed_ref, query_ref, key_ref, value_ref, cotangent_ref, taps_ref, arrived, *, devices, share
 ):
     sources = (query_hbm, key_hbm, value_hbm, taps_hbm, cotangent_hbm)
     targets = (query_ref, key_ref, value_ref, taps_ref, cotangent_ref)
@@ -212,7 +212,7 @@
                 cotangent_ref[at] * query_ref[at],
             )
             for a, slab in enumerate(slabs):
-                out_ref[pl.ds((a * share + c) * runs + r, devices, stride=stride), :] = slab
+                packed_ref[pl.ds((a * share + c) * runs + r, devices, stride=stride), :] = slab
 
 
 def unpack_kernel(
@@ -332,6 +332,7 @@
     full_len = tokens * devices
     scale = 1.0 / (full_len * math.sqrt(full_len))
     packed_shape = jax.ShapeDtypeStruct((channels * 3 * tokens // LANES, LANES), jnp.float32)
+    shape = jax.ShapeDtypeStruct((channels, tokens), jnp.float32)
     sizes = {"devices": devices, "share": share}
 
     def call(kernel, outs, *operands, space=pltpu.VMEM, scratch=()):
@@ -357,15 +358,16 @@
         pltpu.with_memory_space_constraint(x, pltpu.HBM)
         for x in (query_proj, key_proj, value_proj, filter_taps, out_cotangent)
     ]
-    landing = [pltpu.VMEM((channels, tokens), jnp.float32) for _ in inputs]
-    landing.append(pltpu.SemaphoreType.DMA((share, len(inputs))))
-    packed = call(pack_kernel, packed_shape, *inputs, space=pltpu.HBM, scratch=landing)
+    packed, *gates = call(
+        pack_kernel,
+        [packed_shape, *[shape] * 4],
+        *inputs,
+        space=pltpu.HBM,
+        scratch=[pltpu.VMEM((channels, tokens), jnp.float32), pltpu.SemaphoreType.DMA((share, len(inputs)))],
+    )
     tables = [jnp.asarray(table) for table in transform_tables(rows, scale)]
     results = call(channels_kernel, packed_shape, exchange(packed), *tables)
-    outs = [jax.ShapeDtypeStruct((channels, tokens), jnp.float32)] * 5
-    return tuple(
-        call(unpack_kernel, outs, exchange(results), query_proj, key_proj, value_proj, out_cotangent)
-    )
+    return tuple(call(unpack_kernel, [shape] * 5, exchange(results), *gates))
 
 
 def per_device(query_proj, key_proj, value_proj, filter_taps, out_cotangent):

time: 25.7 us -> 25.5 us (level)
  no operation moved by 1% of the time
where the time goes in v4:
time: 25.5 us; the launch traced here: 25.3 us
  blocking collectives  21.5 us (84%)
  Pallas kernels  2.96 us (12%)
  between operations  0.71 us (3%)
    all_to_all x2, blocking collectives, exchange(): lax.all_to_all(blocks, 'seq', split_axis=0, concat_axis=0, tiled=True, ax...  21.5 us
    pallas_call x3, Pallas kernels, call(): pl.pallas_call(lambda *refs: kernel(*refs, **sizes), name=kernel.__name__...  2.96 us

profile of v4, /device:TPU:0, one launch (start us, length us, event | category | flops | bytes accessed | tf_op | source)
XLA Modules:
  0.0 25.3 jit_solution(14265449278746775846)
XLA Ops:
  0.6 0.0 copy-start.4
  0.6 1.1 %pack_kernel.1 = (f32[384,128]{1,0:T(8,128)S(1)}, f32[16,1024]{1,0:T(8,128)S(1)}, f32[16,1024]{1,0:T(8,128)S(1)}, f32[16,1024]{1,0:T(8,128)S(1)}, f32[16,1024]{1,0:T(8,128)S(1)}) custom-call(f32[16,1024]{1,0:T(8,128)} %refs_0_.1, f32[16,1024]{1,0:T(8,128)} %refs_1_.2, f32[16,1024]{1,0:T(8,128)} %refs_2_.2, f32[16,1024]{1,0:T(8,128)} %refs_3_.2, ...), custom_call_target="tpu_custom_call" | custom-call | tf_op jit(solution)/shard_map/pack_kernel/pallas_call | solution.py:340
  1.7 0.0 copy-start
  1.7 0.0 copy-start.1
  1.7 0.0 copy-start.2
  1.7 0.0 copy-start.3
  1.8 12.1 %all_to_all.10 = f32[8,48,128]{2,1,0:T(8,128)S(1)} all-to-all(f32[8,48,128]{2,1,0:T(8,128)S(1)} %bitcast.7), channel_id=1, replica_groups={{20,16,12,28,8,4,0,24},{21,17,13,29,9,5,1,25},{22,18,14,30,10,6,2,26},{..., dimensions={0} | all-to-all | bytes 393216 | tf_op jit(solution)/shard_map/all_to_all | solution.py:352
  13.9 0.0 copy-done.4
  13.9 0.0 copy-done
  13.9 0.0 copy-done.1
  13.9 0.0 copy-done.2
  13.9 0.0 copy-done.3
  13.9 1.1 %channels_kernel.1 = f32[384,128]{1,0:T(8,128)S(1)} custom-call(f32[384,128]{1,0:T(8,128)S(1)} %bitcast.5, bf16[128,192]{1,0:T(8,128)(2,1)S(1)} %copy-done.4, f32[64,256]{1,0:T(8,128)S(1)} %copy-done.3, bf16[256,256]{1,0:T(8,128)(2,1)S(1)} %copy-done.1, bf16[256,256]{1,0:T(8,128)(2,1)S(1)} %copy-done, bf16[128,256]{1,0:T(8,128)(2,1)S(1)} %copy-done.2), custom_call_target="tpu_custom_call" | custom-call | tf_op jit(solution)/shard_map/channels_kernel/pallas_call | solution.py:340
  15.1 9.4 %all_to_all.11 = f32[8,48,128]{2,1,0:T(8,128)S(1)} all-to-all(f32[8,48,128]{2,1,0:T(8,128)S(1)} %bitcast.6), channel_id=1, replica_groups={{20,16,12,28,8,4,0,24},{21,17,13,29,9,5,1,25},{22,18,14,30,10,6,2,26},{..., dimensions={0} | all-to-all | bytes 393216 | tf_op jit(solution)/shard_map/all_to_all | solution.py:352
  24.5 0.8 %unpack_kernel.1 = (f32[16,1024]{1,0:T(8,128)}, f32[16,1024]{1,0:T(8,128)}, f32[16,1024]{1,0:T(8,128)}, f32[16,1024]{1,0:T(8,128)}, f32[16,1024]{1,0:T(8,128)}) custom-call(f32[384,128]{1,0:T(8,128)S(1)} %bitcast.4, f32[16,1024]{1,0:T(8,128)S(1)} %get-tuple-element.11.refs_1_, f32[16,1024]{1,0:T(8,128)S(1)} %get-tuple-element.12.refs_2_, ...), custom_call_target="tpu_custom_call" | custom-call | tf_op jit(solution)/shard_map/unpack_kernel/pallas_call | solution.py:340
Async XLA Ops:
  0.6 13.3 %copy-start.4 = (bf16[128,192]{1,0:T(8,128)(2,1)S(1)}, bf16[128,192]{1,0:T(8,128)(2,1)}, u32[]{:S(2)}) copy-start(bf16[128,192]{1,0:T(8,128)(2,1)} %constant.10.clone.refs_1_) | copy-start | bytes 147460
  1.7 12.2 %copy-start = (bf16[256,256]{1,0:T(8,128)(2,1)S(1)}, bf16[256,256]{1,0:T(8,128)(2,1)}, u32[]{:S(2)}) copy-start(bf16[256,256]{1,0:T(8,128)(2,1)} %constant.13.clone.refs_4_) | copy-start | bytes 393220
  1.7 12.2 %copy-start.1 = (bf16[256,256]{1,0:T(8,128)(2,1)S(1)}, bf16[256,256]{1,0:T(8,128)(2,1)}, u32[]{:S(2)}) copy-start(bf16[256,256]{1,0:T(8,128)(2,1)} %constant.12.clone.refs_3_) | copy-start | bytes 393220
  1.7 12.2 %copy-start.2 = (bf16[128,256]{1,0:T(8,128)(2,1)S(1)}, bf16[128,256]{1,0:T(8,128)(2,1)}, u32[]{:S(2)}) copy-start(bf16[128,256]{1,0:T(8,128)(2,1)} %constant.14.clone.refs_5_) | copy-start | bytes 196612
  1.7 12.2 %copy-start.3 = (f32[64,256]{1,0:T(8,128)S(1)}, f32[64,256]{1,0:T(8,128)}, u32[]{:S(2)}) copy-start(f32[64,256]{1,0:T(8,128)} %constant.11.clone.refs_2_) | copy-start | bytes 196612

commit v5 on v4

--- a/solution.py
+++ b/solution.py
@@ -260,33 +260,6 @@
 
     turn_real = turn_ref[:, :LANES]
     turn_imag = turn_ref[:, LANES:]
-    sequences = jnp.concatenate(
-        [
-            jnp.concatenate(
-                [packed_ref[pl.ds((order.index(s) * items + n) * runs, runs), :] for s in range(devices)],
-                axis=0,
-            )
-            for n in range(items)
-        ],
-        axis=1,
-    )
-    first = dot(row_ref[...], columns(sequences))
-    turned = []
-    for n in range(items):
-        real = first[:rows, n * LANES : (n + 1) * LANES]
-        imag = first[rows:, n * LANES : (n + 1) * LANES]
-        turned.append(
-            jnp.concatenate(
-                [real * turn_real - imag * turn_imag, real * turn_imag + imag * turn_real], axis=1
-            )
-        )
-    spectra = along_lanes(jnp.concatenate(turned, axis=0), 0)
-    size = share * rows
-    gated, taps, weighted = (
-        (spectra[a * size : (a + 1) * size, :LANES], spectra[a * size : (a + 1) * size, LANES:])
-        for a in range(3)
-    )
-
     def product(left, right):
         return jnp.concatenate(
             [left[0] * right[0] - left[1] * right[1], left[0] * right[1] + left[1] * right[0]], axis=1
@@ -297,27 +270,60 @@
             [left[0] * right[0] + left[1] * right[1], left[0] * right[1] - left[1] * right[0]], axis=1
         )
 
-    spectra = jnp.concatenate(
-        [product(taps, gated), against(taps, weighted), against(gated, weighted)], axis=0
-    )
-    bins = along_lanes(spectra, 1)
-    turned = []
-    for n in range(items):
-        real = bins[n * rows : (n + 1) * rows, :LANES]
-        imag = bins[n * rows : (n + 1) * rows, LANES:]
-        turned.append(
-            jnp.concatenate(
-                [real * turn_real + imag * turn_imag, imag * turn_real - real * turn_imag], axis=0
-            )
+    def first_of(a):
+        sequences = jnp.concatenate(
+            [
+                jnp.concatenate(
+                    [packed_ref[pl.ds((order.index(s) * items + n) * runs, runs), :] for s in range(devices)],
+                    axis=0,
+                )
+                for n in range(a * share, (a + 1) * share)
+            ],
+            axis=1,
         )
-    high, low = halves(jnp.concatenate(turned, axis=1))
-    both = dot(back_ref[...], jnp.concatenate([high, low], axis=0))
-    results = both[:rows] + both[rows:]
-    for n in range(items):
-        for s in range(devices):
-            out_ref[pl.ds((order.index(s) * items + n) * runs, runs), :] = results[
-                s * runs : (s + 1) * runs, n * LANES : (n + 1) * LANES
-            ]
+        return dot(row_ref[...], columns(sequences))
+
+    def lines_of(first):
+        turned = []
+        for c in range(share):
+            real = first[:rows, c * LANES : (c + 1) * LANES]
+            imag = first[rows:, c * LANES : (c + 1) * LANES]
+            turned.append(
+                jnp.concatenate(
+                    [real * turn_real - imag * turn_imag, real * turn_imag + imag * turn_real], axis=1
+                )
+            )
+        lines = along_lanes(jnp.concatenate(turned, axis=0), 0)
+        return lines[:, :LANES], lines[:, LANES:]
+
+    def results_of(bins):
+        turned = []
+        for c in range(share):
+            real = bins[c * rows : (c + 1) * rows, :LANES]
+            imag = bins[c * rows : (c + 1) * rows, LANES:]
+            turned.append(
+                jnp.concatenate(
+                    [real * turn_real + imag * turn_imag, imag * turn_real - real * turn_imag], axis=0
+                )
+            )
+        high, low = halves(jnp.concatenate(turned, axis=1))
+        return dot(back_ref[...], jnp.concatenate([high, low], axis=0))
+
+    def store(a, both):
+        results = both[:rows] + both[rows:]
+        for c in range(share):
+            for s in range(devices):
+                out_ref[pl.ds((order.index(s) * items + a * share + c) * runs, runs), :] = results[
+                    s * runs : (s + 1) * runs, c * LANES : (c + 1) * LANES
+                ]
+
+    firsts = [first_of(a) for a in range(3)]
+    gated, taps, weighted = [lines_of(first) for first in firsts]
+    spectra = (product(taps, gated), against(taps, weighted), against(gated, weighted))
+    bins = [along_lanes(spectrum, 1) for spectrum in spectra]
+    results = [results_of(values) for values in bins]
+    for a, both in enumerate(results):
+        store(a, both)
 
 
 def in_vmem(count):

time: 25.5 us -> 25.3 us (level)
  no operation moved by 1% of the time
where the time goes in v5:
time: 25.3 us; the launch traced here: 25.1 us
  blocking collectives  21.5 us (85%)
  Pallas kernels  2.77 us (11%)
  between operations  0.71 us (3%)
    all_to_all x2, blocking collectives, exchange(): lax.all_to_all(blocks, 'seq', split_axis=0, concat_axis=0, tiled=True, ax...  21.5 us
    pallas_call x3, Pallas kernels, call(): pl.pallas_call(lambda *refs: kernel(*refs, **sizes), name=kernel.__name__...  2.77 us

profile of v5, /device:TPU:0, one launch (start us, length us, event | category | flops | bytes accessed | tf_op | source)
XLA Modules:
  0.0 25.1 jit_solution(10849672990420807686)
XLA Ops:
  0.6 0.0 copy-start.4
  0.6 1.1 %pack_kernel.1 = (f32[384,128]{1,0:T(8,128)S(1)}, f32[16,1024]{1,0:T(8,128)S(1)}, f32[16,1024]{1,0:T(8,128)S(1)}, f32[16,1024]{1,0:T(8,128)S(1)}, f32[16,1024]{1,0:T(8,128)S(1)}) custom-call(f32[16,1024]{1,0:T(8,128)} %refs_0_.1, f32[16,1024]{1,0:T(8,128)} %refs_1_.2, f32[16,1024]{1,0:T(8,128)} %refs_2_.2, f32[16,1024]{1,0:T(8,128)} %refs_3_.2, ...), custom_call_target="tpu_custom_call" | custom-call | tf_op jit(solution)/shard_map/pack_kernel/pallas_call | solution.py:346
  1.7 0.0 copy-start
  1.7 0.0 copy-start.1
  1.7 0.0 copy-start.2
  1.7 0.0 copy-start.3
  1.8 12.1 %all_to_all.10 = f32[8,48,128]{2,1,0:T(8,128)S(1)} all-to-all(f32[8,48,128]{2,1,0:T(8,128)S(1)} %bitcast.7), channel_id=1, replica_groups={{20,16,12,28,8,4,0,24},{21,17,13,29,9,5,1,25},{22,18,14,30,10,6,2,26},{..., dimensions={0} | all-to-all | bytes 393216 | tf_op jit(solution)/shard_map/all_to_all | solution.py:358
  13.9 0.0 copy-done.4
  13.9 0.0 copy-done
  13.9 0.0 copy-done.1
  13.9 0.0 copy-done.2
  13.9 0.0 copy-done.3
  13.9 0.9 %channels_kernel.1 = f32[384,128]{1,0:T(8,128)S(1)} custom-call(f32[384,128]{1,0:T(8,128)S(1)} %bitcast.5, bf16[128,192]{1,0:T(8,128)(2,1)S(1)} %copy-done.4, f32[64,256]{1,0:T(8,128)S(1)} %copy-done.3, bf16[256,256]{1,0:T(8,128)(2,1)S(1)} %copy-done.1, bf16[256,256]{1,0:T(8,128)(2,1)S(1)} %copy-done, bf16[128,256]{1,0:T(8,128)(2,1)S(1)} %copy-done.2), custom_call_target="tpu_custom_call" | custom-call | tf_op jit(solution)/shard_map/channels_kernel/pallas_call | solution.py:346
  14.9 9.4 %all_to_all.11 = f32[8,48,128]{2,1,0:T(8,128)S(1)} all-to-all(f32[8,48,128]{2,1,0:T(8,128)S(1)} %bitcast.6), channel_id=1, replica_groups={{20,16,12,28,8,4,0,24},{21,17,13,29,9,5,1,25},{22,18,14,30,10,6,2,26},{..., dimensions={0} | all-to-all | bytes 393216 | tf_op jit(solution)/shard_map/all_to_all | solution.py:358
  24.3 0.8 %unpack_kernel.1 = (f32[16,1024]{1,0:T(8,128)}, f32[16,1024]{1,0:T(8,128)}, f32[16,1024]{1,0:T(8,128)}, f32[16,1024]{1,0:T(8,128)}, f32[16,1024]{1,0:T(8,128)}) custom-call(f32[384,128]{1,0:T(8,128)S(1)} %bitcast.4, f32[16,1024]{1,0:T(8,128)S(1)} %get-tuple-element.11.refs_1_, f32[16,1024]{1,0:T(8,128)S(1)} %get-tuple-element.12.refs_2_, ...), custom_call_target="tpu_custom_call" | custom-call | tf_op jit(solution)/shard_map/unpack_kernel/pallas_call | solution.py:346
Async XLA Ops:
  0.6 13.3 %copy-start.4 = (bf16[128,192]{1,0:T(8,128)(2,1)S(1)}, bf16[128,192]{1,0:T(8,128)(2,1)}, u32[]{:S(2)}) copy-start(bf16[128,192]{1,0:T(8,128)(2,1)} %constant.10.clone.refs_1_) | copy-start | bytes 147460
  1.7 12.2 %copy-start = (bf16[256,256]{1,0:T(8,128)(2,1)S(1)}, bf16[256,256]{1,0:T(8,128)(2,1)}, u32[]{:S(2)}) copy-start(bf16[256,256]{1,0:T(8,128)(2,1)} %constant.13.clone.refs_4_) | copy-start | bytes 393220
  1.7 12.2 %copy-start.1 = (bf16[256,256]{1,0:T(8,128)(2,1)S(1)}, bf16[256,256]{1,0:T(8,128)(2,1)}, u32[]{:S(2)}) copy-start(bf16[256,256]{1,0:T(8,128)(2,1)} %constant.12.clone.refs_3_) | copy-start | bytes 393220
  1.7 12.2 %copy-start.2 = (bf16[128,256]{1,0:T(8,128)(2,1)S(1)}, bf16[128,256]{1,0:T(8,128)(2,1)}, u32[]{:S(2)}) copy-start(bf16[128,256]{1,0:T(8,128)(2,1)} %constant.14.clone.refs_5_) | copy-start | bytes 196612
  1.7 12.2 %copy-start.3 = (f32[64,256]{1,0:T(8,128)S(1)}, f32[64,256]{1,0:T(8,128)}, u32[]{:S(2)}) copy-start(f32[64,256]{1,0:T(8,128)} %constant.11.clone.refs_2_) | copy-start | bytes 196612

commit v6 on v5

--- a/solution.py
+++ b/solution.py
@@ -156,7 +156,7 @@
     lane = np.arange(LANES)
     lane_angle = -2.0 * math.pi * ((lane[:, None] * lane[None, :]) % LANES) / LANES
     cos_lane, sin_lane = (np.cos(lane_angle), np.sin(lane_angle))
-    lane_table = np.block([[cos_lane, sin_lane], [-sin_lane, cos_lane]])
+    lane_table = np.concatenate([cos_lane, sin_lane], axis=1)
     row_high, row_low = halves(row_table)
     back_high, back_low = halves(row_table.T * scale)
     lane_high, lane_low = halves(lane_table)
@@ -172,13 +172,8 @@
 
 
 def exchange_order(devices):
-    middle = min(devices // 2 + 1, devices - 1)
-    order = list(range(middle, -1, -1))
-    above = list(range(devices - 1, middle, -1))
-    step = len(order) // max(len(above), 1)
-    for i, device in enumerate(above):
-        order.insert((i + 1) * step + i, device)
-    return order
+    eighth = devices // 8
+    return [part * eighth + i for part in (5, 2, 3, 7, 1, 4, 0, 6) for i in range(eighth)]
 
 
 def pack_kernel(
@@ -252,12 +247,21 @@
         high, low = halves(values)
         return jnp.concatenate([high, low, high], axis=0)
 
-    def along_lanes(values, right_dim):
+    def along_lanes(values, high_table, low_table):
         high, low = halves(values)
         size = values.shape[0]
-        both = dot(jnp.concatenate([high, low], axis=0), lane_high_ref[...], right_dim)
-        return both[:size] + both[size:] + dot(high, lane_low_ref[...], right_dim)
-
+        both = dot(jnp.concatenate([high, low], axis=0), high_table)
+        return both[:size] + both[size:] + dot(high, low_table)
+
+    def square(table_ref, conjugate):
+        cosines, sines = (table_ref[:, :LANES], table_ref[:, LANES:])
+        above, below = (-sines, sines) if conjugate else (sines, -sines)
+        return jnp.concatenate(
+            [jnp.concatenate([cosines, above], axis=1), jnp.concatenate([below, cosines], axis=1)], axis=0
+        )
+
+    forward = (square(lane_high_ref, False), square(lane_low_ref, False))
+    backward = (square(lane_high_ref, True), square(lane_low_ref, True))
     turn_real = turn_ref[:, :LANES]
     turn_imag = turn_ref[:, LANES:]
     def product(left, right):
@@ -293,7 +297,7 @@
                     [real * turn_real - imag * turn_imag, real * turn_imag + imag * turn_real], axis=1
                 )
             )
-        lines = along_lanes(jnp.concatenate(turned, axis=0), 0)
+        lines = along_lanes(jnp.concatenate(turned, axis=0), *forward)
         return lines[:, :LANES], lines[:, LANES:]
 
     def results_of(bins):
@@ -320,7 +324,7 @@
     firsts = [first_of(a) for a in range(3)]
     gated, taps, weighted = [lines_of(first) for first in firsts]
     spectra = (product(taps, gated), against(taps, weighted), against(gated, weighted))
-    bins = [along_lanes(spectrum, 1) for spectrum in spectra]
+    bins = [along_lanes(spectrum, *backward) for spectrum in spectra]
     results = [results_of(values) for values in bins]
     for a, both in enumerate(results):
         store(a, both)

time: 25.3 us -> 25.1 us (level)
  no operation moved by 1% of the time
where the time goes in v6:
time: 25.1 us; the launch traced here: 24.8 us
  blocking collectives  21.4 us (85%)
  Pallas kernels  2.73 us (11%)
  between operations  0.71 us (3%)
    all_to_all x2, blocking collectives, exchange(): lax.all_to_all(blocks, 'seq', split_axis=0, concat_axis=0, tiled=True, ax...  21.4 us
    pallas_call x3, Pallas kernels, call(): pl.pallas_call(lambda *refs: kernel(*refs, **sizes), name=kernel.__name__...  2.73 us

profile of v6, /device:TPU:0, one launch (start us, length us, event | category | flops | bytes accessed | tf_op | source)
XLA Modules:
  0.0 24.8 jit_solution(4296819114870402227)
XLA Ops:
  0.6 1.0 %pack_kernel.1 = (f32[384,128]{1,0:T(8,128)S(1)}, f32[16,1024]{1,0:T(8,128)S(1)}, f32[16,1024]{1,0:T(8,128)S(1)}, f32[16,1024]{1,0:T(8,128)S(1)}, f32[16,1024]{1,0:T(8,128)S(1)}) custom-call(f32[16,1024]{1,0:T(8,128)} %refs_0_.1, f32[16,1024]{1,0:T(8,128)} %refs_1_.2, f32[16,1024]{1,0:T(8,128)} %refs_2_.2, f32[16,1024]{1,0:T(8,128)} %refs_3_.2, ...), custom_call_target="tpu_custom_call" | custom-call | tf_op jit(solution)/shard_map/pack_kernel/pallas_call | solution.py:350
  1.7 0.0 copy-start
  1.7 0.0 copy-start.1
  1.7 0.0 copy-start.2
  1.7 0.0 copy-start.3
  1.7 0.0 copy-start.4
  1.7 12.7 %all_to_all.10 = f32[8,48,128]{2,1,0:T(8,128)S(1)} all-to-all(f32[8,48,128]{2,1,0:T(8,128)S(1)} %bitcast.7), channel_id=1, replica_groups={{20,8,12,28,4,16,0,24},{21,9,13,29,5,17,1,25},{22,10,14,30,6,18,2,26},{..., dimensions={0} | all-to-all | bytes 393216 | tf_op jit(solution)/shard_map/all_to_all | solution.py:362
  14.4 0.0 copy-done
  14.4 0.0 copy-done.1
  14.4 0.0 copy-done.2
  14.4 0.0 copy-done.3
  14.4 0.0 copy-done.4
  14.4 0.9 %channels_kernel.1 = f32[384,128]{1,0:T(8,128)S(1)} custom-call(f32[384,128]{1,0:T(8,128)S(1)} %bitcast.5, bf16[128,192]{1,0:T(8,128)(2,1)S(1)} %copy-done.4, f32[64,256]{1,0:T(8,128)S(1)} %copy-done.3, bf16[128,256]{1,0:T(8,128)(2,1)S(1)} %copy-done.2, bf16[128,256]{1,0:T(8,128)(2,1)S(1)} %copy-done.1, bf16[128,256]{1,0:T(8,128)(2,1)S(1)} %copy-done), custom_call_target="tpu_custom_call" | custom-call | tf_op jit(solution)/shard_map/channels_kernel/pallas_call | solution.py:350
  15.4 8.7 %all_to_all.11 = f32[8,48,128]{2,1,0:T(8,128)S(1)} all-to-all(f32[8,48,128]{2,1,0:T(8,128)S(1)} %bitcast.6), channel_id=1, replica_groups={{20,8,12,28,4,16,0,24},{21,9,13,29,5,17,1,25},{22,10,14,30,6,18,2,26},{..., dimensions={0} | all-to-all | bytes 393216 | tf_op jit(solution)/shard_map/all_to_all | solution.py:362
  24.1 0.8 %unpack_kernel.1 = (f32[16,1024]{1,0:T(8,128)}, f32[16,1024]{1,0:T(8,128)}, f32[16,1024]{1,0:T(8,128)}, f32[16,1024]{1,0:T(8,128)}, f32[16,1024]{1,0:T(8,128)}) custom-call(f32[384,128]{1,0:T(8,128)S(1)} %bitcast.4, f32[16,1024]{1,0:T(8,128)S(1)} %get-tuple-element.11.refs_1_, f32[16,1024]{1,0:T(8,128)S(1)} %get-tuple-element.12.refs_2_, ...), custom_call_target="tpu_custom_call" | custom-call | tf_op jit(solution)/shard_map/unpack_kernel/pallas_call | solution.py:350
Async XLA Ops:
  1.7 12.7 %copy-start = (bf16[128,256]{1,0:T(8,128)(2,1)S(1)}, bf16[128,256]{1,0:T(8,128)(2,1)}, u32[]{:S(2)}) copy-start(bf16[128,256]{1,0:T(8,128)(2,1)} %constant.14.clone.refs_5_) | copy-start | bytes 196612
  1.7 12.7 %copy-start.1 = (bf16[128,256]{1,0:T(8,128)(2,1)S(1)}, bf16[128,256]{1,0:T(8,128)(2,1)}, u32[]{:S(2)}) copy-start(bf16[128,256]{1,0:T(8,128)(2,1)} %constant.13.clone.refs_4_) | copy-start | bytes 196612
  1.7 12.7 %copy-start.2 = (bf16[128,256]{1,0:T(8,128)(2,1)S(1)}, bf16[128,256]{1,0:T(8,128)(2,1)}, u32[]{:S(2)}) copy-start(bf16[128,256]{1,0:T(8,128)(2,1)} %constant.12.clone.refs_3_) | copy-start | bytes 196612
  1.7 12.7 %copy-start.3 = (f32[64,256]{1,0:T(8,128)S(1)}, f32[64,256]{1,0:T(8,128)}, u32[]{:S(2)}) copy-start(f32[64,256]{1,0:T(8,128)} %constant.11.clone.refs_2_) | copy-start | bytes 196612
  1.7 12.7 %copy-start.4 = (bf16[128,192]{1,0:T(8,128)(2,1)S(1)}, bf16[128,192]{1,0:T(8,128)(2,1)}, u32[]{:S(2)}) copy-start(bf16[128,192]{1,0:T(8,128)(2,1)} %constant.10.clone.refs_1_) | copy-start | bytes 147460

commit v7 on v6

--- a/solution.py
+++ b/solution.py
@@ -165,9 +165,7 @@
         turn,
         lane_high,
         lane_low,
-        np.concatenate(
-            [np.concatenate([back_high, back_high], axis=1), np.concatenate([back_low, np.zeros_like(back_low)], axis=1)]
-        ),
+        np.concatenate([back_high, back_low], axis=1),
     )
 
 
@@ -262,6 +260,14 @@
 
     forward = (square(lane_high_ref, False), square(lane_low_ref, False))
     backward = (square(lane_high_ref, True), square(lane_low_ref, True))
+    back_high, back_low = (back_ref[:, : 2 * rows], back_ref[:, 2 * rows :])
+    back_table = jnp.concatenate(
+        [
+            jnp.concatenate([back_high, back_high], axis=1),
+            jnp.concatenate([back_low, jnp.zeros_like(back_low)], axis=1),
+        ],
+        axis=0,
+    )
     turn_real = turn_ref[:, :LANES]
     turn_imag = turn_ref[:, LANES:]
     def product(left, right):
@@ -311,7 +317,7 @@
                 )
             )
         high, low = halves(jnp.concatenate(turned, axis=1))
-        return dot(back_ref[...], jnp.concatenate([high, low], axis=0))
+        return dot(back_table, jnp.concatenate([high, low], axis=0))
 
     def store(a, both):
         results = both[:rows] + both[rows:]

time: 25.1 us -> 25.1 us (level)
  no operation moved by 1% of the time
where the time goes in v7:
time: 25.1 us; the launch traced here: 24.8 us
  blocking collectives  21.4 us (85%)
  Pallas kernels  2.73 us (11%)
  between operations  0.71 us (3%)
    all_to_all x2, blocking collectives, exchange(): lax.all_to_all(blocks, 'seq', split_axis=0, concat_axis=0, tiled=True, ax...  21.4 us
    pallas_call x3, Pallas kernels, call(): pl.pallas_call(lambda *refs: kernel(*refs, **sizes), name=kernel.__name__...  2.73 us

profile of v7, /device:TPU:0, one launch (start us, length us, event | category | flops | bytes accessed | tf_op | source)
XLA Modules:
  0.0 24.8 jit_solution(8527391959373862299)
XLA Ops:
  0.6 1.0 %pack_kernel.1 = (f32[384,128]{1,0:T(8,128)S(1)}, f32[16,1024]{1,0:T(8,128)S(1)}, f32[16,1024]{1,0:T(8,128)S(1)}, f32[16,1024]{1,0:T(8,128)S(1)}, f32[16,1024]{1,0:T(8,128)S(1)}) custom-call(f32[16,1024]{1,0:T(8,128)} %refs_0_.1, f32[16,1024]{1,0:T(8,128)} %refs_1_.2, f32[16,1024]{1,0:T(8,128)} %refs_2_.2, f32[16,1024]{1,0:T(8,128)} %refs_3_.2, ...), custom_call_target="tpu_custom_call" | custom-call | tf_op jit(solution)/shard_map/pack_kernel/pallas_call | solution.py:356
  1.7 0.0 copy-start
  1.7 0.0 copy-start.1
  1.7 0.0 copy-start.2
  1.7 0.0 copy-start.3
  1.7 0.0 copy-start.4
  1.7 12.7 %all_to_all.10 = f32[8,48,128]{2,1,0:T(8,128)S(1)} all-to-all(f32[8,48,128]{2,1,0:T(8,128)S(1)} %bitcast.7), channel_id=1, replica_groups={{20,8,12,28,4,16,0,24},{21,9,13,29,5,17,1,25},{22,10,14,30,6,18,2,26},{..., dimensions={0} | all-to-all | bytes 393216 | tf_op jit(solution)/shard_map/all_to_all | solution.py:368
  14.4 0.0 copy-done
  14.4 0.0 copy-done.1
  14.4 0.0 copy-done.2
  14.4 0.0 copy-done.3
  14.4 0.0 copy-done.4
  14.4 0.9 %channels_kernel.1 = f32[384,128]{1,0:T(8,128)S(1)} custom-call(f32[384,128]{1,0:T(8,128)S(1)} %bitcast.5, bf16[128,192]{1,0:T(8,128)(2,1)S(1)} %copy-done.3, f32[64,256]{1,0:T(8,128)S(1)} %copy-done.2, bf16[128,256]{1,0:T(8,128)(2,1)S(1)} %copy-done.1, bf16[128,256]{1,0:T(8,128)(2,1)S(1)} %copy-done, bf16[64,256]{1,0:T(8,128)(2,1)S(1)} %copy-done.4), custom_call_target="tpu_custom_call" | custom-call | tf_op jit(solution)/shard_map/channels_kernel/pallas_call | solution.py:356
  15.4 8.7 %all_to_all.11 = f32[8,48,128]{2,1,0:T(8,128)S(1)} all-to-all(f32[8,48,128]{2,1,0:T(8,128)S(1)} %bitcast.6), channel_id=1, replica_groups={{20,8,12,28,4,16,0,24},{21,9,13,29,5,17,1,25},{22,10,14,30,6,18,2,26},{..., dimensions={0} | all-to-all | bytes 393216 | tf_op jit(solution)/shard_map/all_to_all | solution.py:368
  24.1 0.8 %unpack_kernel.1 = (f32[16,1024]{1,0:T(8,128)}, f32[16,1024]{1,0:T(8,128)}, f32[16,1024]{1,0:T(8,128)}, f32[16,1024]{1,0:T(8,128)}, f32[16,1024]{1,0:T(8,128)}) custom-call(f32[384,128]{1,0:T(8,128)S(1)} %bitcast.4, f32[16,1024]{1,0:T(8,128)S(1)} %get-tuple-element.11.refs_1_, f32[16,1024]{1,0:T(8,128)S(1)} %get-tuple-element.12.refs_2_, ...), custom_call_target="tpu_custom_call" | custom-call | tf_op jit(solution)/shard_map/unpack_kernel/pallas_call | solution.py:356
Async XLA Ops:
  1.7 12.7 %copy-start = (bf16[128,256]{1,0:T(8,128)(2,1)S(1)}, bf16[128,256]{1,0:T(8,128)(2,1)}, u32[]{:S(2)}) copy-start(bf16[128,256]{1,0:T(8,128)(2,1)} %constant.13.clone.refs_4_) | copy-start | bytes 196612
  1.7 12.7 %copy-start.1 = (bf16[128,256]{1,0:T(8,128)(2,1)S(1)}, bf16[128,256]{1,0:T(8,128)(2,1)}, u32[]{:S(2)}) copy-start(bf16[128,256]{1,0:T(8,128)(2,1)} %constant.12.clone.refs_3_) | copy-start | bytes 196612
  1.7 12.7 %copy-start.2 = (f32[64,256]{1,0:T(8,128)S(1)}, f32[64,256]{1,0:T(8,128)}, u32[]{:S(2)}) copy-start(f32[64,256]{1,0:T(8,128)} %constant.11.clone.refs_2_) | copy-start | bytes 196612
  1.7 12.7 %copy-start.3 = (bf16[128,192]{1,0:T(8,128)(2,1)S(1)}, bf16[128,192]{1,0:T(8,128)(2,1)}, u32[]{:S(2)}) copy-start(bf16[128,192]{1,0:T(8,128)(2,1)} %constant.10.clone.refs_1_) | copy-start | bytes 147460
  1.7 12.7 %copy-start.4 = (bf16[64,256]{1,0:T(8,128)(2,1)S(1)}, bf16[64,256]{1,0:T(8,128)(2,1)}, u32[]{:S(2)}) copy-start(bf16[64,256]{1,0:T(8,128)(2,1)} %constant.14.clone.refs_5_) | copy-start | bytes 98308
